TPU v7x, 32 devices: a whole 2x2x4 slice. The times are simulated.
32 devices in a mesh: ty: 16 (over z, y, core), tx: 2 (over x).
Axes of the slice: x: 2, y: 2, z: 4, core: 2. Of those that a mesh axis runs over, the one named last changes fastest.
Arguments:
- ctrl: float32 [16, 2, 512, 640], P('ty', 'tx'), may hold values from -6 to 6
- interp_wt: float32 [16, 2, 4, 128, 384], P('ty', 'tx'), may hold values from -0.3125 to 0.3125
- interp_cols: int32 [16, 2, 4, 384], P('ty', 'tx'), may hold values from 0 to 1023
- conv_wt: float32 [16, 2, 4, 128, 512], P('ty', 'tx'), may hold values from -0.25 to 0.25
- conv_cols: int32 [16, 2, 4, 512], P('ty', 'tx'), may hold values from 0 to 1023
- halo_index: int32 [16, 2, 8, 64], P('ty', 'tx'), may hold values from 0 to 511
- valid: int32 [16, 2], P('ty', 'tx'), may hold values from 256 to 512
Outputs:
- localized: float32 [16, 2, 512, 640], P('ty', 'tx')
Inputs may be any that keep to these rules, and one draw needn't show every extreme that they name: `interp_cols`: indices into a tile's extended subgrid of 1024 rows; repeats are allowed. `conv_cols`: indices into a tile's extended subgrid; repeats are allowed. `halo_index`: owned row indices; repeats are allowed.
All inputs are finite; a program needn't handle non-finite values.
Results may differ from a plain program's by a relative error of at most 0.0001.
Values sent between devices are 32-bit elements; how exact they have to be, the bound alone decides.
A program may use at most 64 MiB of HBM per device.

v0:
```python
import jax
import jax.numpy as jnp
from jax import lax
from jax.sharding import PartitionSpec as P

DIRECTIONS = ((-1, -1), (-1, 0), (-1, 1), (0, -1), (0, 1), (1, -1), (1, 0), (1, 1))


def passed_along(value, axis, steps):
    count = lax.axis_size(axis)
    pairs = [(source, (source + steps) % count) for source in range(count)]
    return lax.ppermute(value, axis, pairs)


def shifted(block, axis, distance):
    devices = range(lax.axis_size(axis))
    route = [(i - distance, i) for i in devices if i - distance in devices]
    return lax.ppermute(block, axis, route)


def move_rows(outgoing, backward):
    offsets = [
        (-row_off, -col_off) if backward else (row_off, col_off) for row_off, col_off in DIRECTIONS
    ]
    received = []
    for slot_id in range(8):
        carried = outgoing[slot_id]
        if offsets[slot_id][1] != 0:
            carried = passed_along(carried, "tx", offsets[slot_id][1])
        if offsets[slot_id][0] != 0:
            carried = shifted(carried, "ty", offsets[slot_id][0])
        received.append(carried)
    return jnp.stack(received)


def block_product(weights, gathered):
    return jnp.einsum("bgc,bcf->bgf", weights, gathered, precision=lax.Precision.HIGHEST)


def adjoint_blocks(weights, cols, values, extent):
    blocks = values.reshape(weights.shape[0], weights.shape[1], values.shape[1])
    contrib = jnp.einsum("bgc,bgf->bcf", weights, blocks, precision=lax.Precision.HIGHEST)
    return jax.ops.segment_sum(
        contrib.reshape(-1, values.shape[1]), cols.reshape(-1), num_segments=extent
    )


def accumulate(contrib, halo_idx, own_rows):
    width = contrib.shape[1]
    slots = contrib[own_rows:].reshape(8, halo_idx.shape[1], width)
    arrived = move_rows(slots, True)
    added = jax.ops.segment_sum(
        arrived.reshape(-1, width), halo_idx.reshape(-1), num_segments=own_rows
    )
    return contrib[:own_rows] + added


def apply_forward(weights, cols, owned, halo_idx):
    own_rows, width = owned.shape
    sends = jnp.take(owned, halo_idx, axis=0)
    slots = move_rows(sends, False).reshape(-1, width)
    extended = jnp.concatenate([owned, slots], axis=0)
    gathered = jnp.take(extended, cols, axis=0)
    return block_product(weights, gathered).reshape(-1, width)


def body(ctrl, interp_wt, interp_cols, conv_wt, conv_cols, halo_index, valid):
    field = ctrl[0, 0]
    grid_rows = field.shape[0]
    iweights = interp_wt[0, 0]
    icolumns = interp_cols[0, 0]
    cweights = conv_wt[0, 0]
    ccolumns = conv_cols[0, 0]
    halo_idx = halo_index[0, 0]
    own_rows = cweights.shape[0] * cweights.shape[1]
    extent = own_rows + 8 * halo_idx.shape[1]
    positions = jnp.arange(grid_rows, dtype=jnp.int32)
    mask = (positions < valid[0, 0]).astype(jnp.float32)[:, None]
    a_ext = adjoint_blocks(iweights, icolumns, field * mask, extent)
    summed = accumulate(a_ext, halo_idx, own_rows)
    b_ext = adjoint_blocks(cweights, ccolumns, summed, extent)
    spread = accumulate(b_ext, halo_idx, own_rows)
    smooth = apply_forward(cweights, ccolumns, spread, halo_idx)
    result = apply_forward(iweights, icolumns, smooth, halo_idx) * mask
    return result[None, None]


def solution(mesh):
    placed = (
        P("ty", "tx", None, None),
        P("ty", "tx", None, None, None),
        P("ty", "tx", None, None),
        P("ty", "tx", None, None, None),
        P("ty", "tx", None, None),
        P("ty", "tx", None, None),
        P("ty", "tx"),
    )
    return jax.shard_map(
        body, mesh=mesh, in_specs=placed, out_specs=P("ty", "tx", None, None), check_vma=False
    )
```

profile of v0, /device:TPU:1, one launch (start us, length us, event | category | flops | bytes accessed | tf_op | source)
XLA Modules:
  0.0 257.9 jit_solution(8640581386159077707)
XLA Ops:
  1.5 6.8 %fusion.8 = f32[4,640,384]{1,2,0:T(8,128)} fusion(f32[4,128,640]{2,1,0:T(8,128)} %bitcast.172, f32[1,1,4,128,384]{4,3,2,1,0:T(8,128)} %param.10, f32[4,128]{1,0:T(4,128)S(1)} %fusion.21), kind=kOutput, calls=%fused_computation.18 | convolution fusion | flops 1510277120 | bytes 6031360 | tf_op jit(solution)/shard_map/bgc,bgf->bcf/dot_general | solution.py:42
  8.2 12.8 %scatter_custom_fusion = f32[1024,640]{1,0:T(8,128)} fusion(s32[1536]{0:T(1024)S(1)} %reshape.219, f32[1536,640]{1,0:T(8,128)} %bitcast.167, f32[]{:T(128)} %constant.40.clone.1), kind=kCustom, calls=%fused_computation.22 | custom fusion | flops 983040 | bytes 2621952 | tf_op jit(solution)/shard_map/scatter-add | solution.py:43
  22.5 2.1 collective-permute-start
  24.6 4.0 %collective-permute-start.2 = (f32[64,640]{1,0:T(8,128)S(1)}, f32[64,640]{1,0:T(8,128)}, u32[]{:S(2)}, u32[]{:S(2)}) collective-permute-start(f32[64,640]{1,0:T(8,128)S(1)} %get-tuple-element.20), channel_id=1, source_target_pairs={{0,2},{2,4},{4,6},{6,8},{8,10},{10,12},{12,14},{14,16},{16,18},{18... | collective-permute-start | bytes 491528 | tf_op jit(solution)/shard_map/ppermute | solution.py:18
  30.9 2.5 collective-permute-start.1
  33.4 2.2 collective-permute-done.1
  37.2 4.9 %collective-permute-start.4 = (f32[64,640]{1,0:T(8,128)}, f32[64,640]{1,0:T(8,128)S(1)}, u32[]{:S(2)}, u32[]{:S(2)}) collective-permute-start(f32[64,640]{1,0:T(8,128)} %collective-permute-done.3), channel_id=1, source_target_pairs={{0,2},{2,4},{4,6},{6,8},{8,10},{10,12},{12,14},{14,16},{16,18},{18... | collective-permute-start | bytes 491528 | tf_op jit(solution)/shard_map/ppermute | solution.py:18
  43.1 2.3 collective-permute-done.7
  45.4 1.9 collective-permute-start.9
  48.1 2.1 collective-permute-start.8
  50.2 1.9 collective-permute-start.11
  54.8 2.1 collective-permute-done.11
  57.9 5.3 %scatter_fusion = f32[512,640]{1,0:T(8,128)S(1)} fusion(f32[512,640]{1,0:T(8,128)S(1)} %slice-done.1, s32[512]{0:T(512)S(1)} %reshape.227, f32[512,640]{1,0:T(8,128)} %bitcast.168), kind=kCustom, calls=%fused_computation.5 | custom fusion | flops 327680 | bytes 3934208 | tf_op jit(solution)/shard_map/scatter-add | solution.py:52
  63.2 6.0 %fusion.15 = f32[4,640,512]{1,2,0:T(8,128)} fusion(f32[4,128,640]{2,1,0:T(8,128)S(1)} %bitcast.160, f32[1,1,4,128,512]{4,3,2,1,0:T(8,128)S(1)} %copy-done), kind=kOutput, calls=%fused_computation.25 | convolution fusion | flops 2013265920 | bytes 7602176 | tf_op jit(solution)/shard_map/bgc,bgf->bcf/dot_general | solution.py:42
  69.2 16.1 %scatter_custom_fusion.2 = f32[1024,640]{1,0:T(8,128)} fusion(s32[2048]{0:T(1024)S(1)} %bitcast.175, f32[2048,640]{1,0:T(8,128)} %bitcast.163, f32[]{:T(128)} %constant.40.clone.1), kind=kCustom, calls=%fused_computation.20 | custom fusion | flops 1310720 | bytes 2621952 | tf_op jit(solution)/shard_map/scatter-add | solution.py:43
  86.9 4.1 %collective-permute-done.12 = f32[64,640]{1,0:T(8,128)S(1)} collective-permute-done((f32[64,640]{1,0:T(8,128)S(1)}, f32[64,640]{1,0:T(8,128)S(1)}, u32[]{:S(2)}, u32[]{:S(2)}) %collective-permute-start.12) | collective-permute-done | bytes 163872 | tf_op jit(solution)/shard_map/ppermute | solution.py:12
  91.0 3.2 %collective-permute-start.13 = (f32[64,640]{1,0:T(8,128)S(1)}, f32[64,640]{1,0:T(8,128)S(1)}, u32[]{:S(2)}, u32[]{:S(2)}) collective-permute-start(f32[64,640]{1,0:T(8,128)S(1)} %collective-permute-done.12), channel_id=1, source_target_pairs={{0,2},{2,4},{4,6},{6,8},{8,10},{10,12},{12,14},{14,16},{16,18},{18... | collective-permute-start | bytes 491528 | tf_op jit(solution)/shard_map/ppermute | solution.py:18
  94.9 3.2 %collective-permute-start.14 = (f32[64,640]{1,0:T(8,128)S(1)}, f32[64,640]{1,0:T(8,128)S(1)}, u32[]{:S(2)}, u32[]{:S(2)}) collective-permute-start(f32[64,640]{1,0:T(8,128)S(1)} %get-tuple-element.12), channel_id=1, source_target_pairs={{0,2},{2,4},{4,6},{6,8},{8,10},{10,12},{12,14},{14,16},{16,18},{18... | collective-permute-start | bytes 491528 | tf_op jit(solution)/shard_map/ppermute | solution.py:18
  104.3 4.6 %collective-permute-start.16 = (f32[64,640]{1,0:T(8,128)S(1)}, f32[64,640]{1,0:T(8,128)S(1)}, u32[]{:S(2)}, u32[]{:S(2)}) collective-permute-start(f32[64,640]{1,0:T(8,128)S(1)} %collective-permute-done.15), channel_id=1, source_target_pairs={{0,2},{2,4},{4,6},{6,8},{8,10},{10,12},{12,14},{14,16},{16,18},{18... | collective-permute-start | bytes 491528 | tf_op jit(solution)/shard_map/ppermute | solution.py:18
  109.0 5.9 %collective-permute-done.19 = f32[64,640]{1,0:T(8,128)S(1)} collective-permute-done((f32[64,640]{1,0:T(8,128)S(1)}, f32[64,640]{1,0:T(8,128)S(1)}, u32[]{:S(2)}, u32[]{:S(2)}) %collective-permute-start.19) | collective-permute-done | bytes 163872 | tf_op jit(solution)/shard_map/ppermute | solution.py:12
  114.9 1.9 collective-permute-start.21
  117.8 2.3 collective-permute-start.20
  120.1 1.9 collective-permute-start.23
  122.1 3.3 %collective-permute-done.20 = f32[64,640]{1,0:T(8,128)S(1)} collective-permute-done((f32[64,640]{1,0:T(8,128)S(1)}, f32[64,640]{1,0:T(8,128)S(1)}, u32[]{:S(2)}, u32[]{:S(2)}) %collective-permute-start.20) | collective-permute-done | bytes 163872 | tf_op jit(solution)/shard_map/ppermute | solution.py:18
  128.4 5.1 %scatter_fusion.1 = f32[512,640]{1,0:T(8,128)S(1)} fusion(f32[512,640]{1,0:T(8,128)S(1)} %slice-done, s32[512]{0:T(512)S(1)} %reshape.227, f32[512,640]{1,0:T(8,128)} %bitcast.169), kind=kCustom, calls=%fused_computation.7 | custom fusion | flops 327680 | bytes 3934208 | tf_op jit(solution)/shard_map/scatter-add | solution.py:52
  133.6 2.6 gather_fusion.2
  138.5 3.4 %collective-permute-done.24 = f32[64,640]{1,0:T(8,128)S(1)} collective-permute-done((f32[64,640]{1,0:T(8,128)S(1)}, f32[64,640]{1,0:T(8,128)S(1)}, u32[]{:S(2)}, u32[]{:S(2)}) %collective-permute-start.24) | collective-permute-done | bytes 163872 | tf_op jit(solution)/shard_map/ppermute | solution.py:12
  141.9 1.9 collective-permute-start.25
  143.9 1.9 collective-permute-start.26
  152.1 1.9 collective-permute-start.28
  154.0 6.4 %collective-permute-done.31 = f32[64,640]{1,0:T(8,128)S(1)} collective-permute-done((f32[64,640]{1,0:T(8,128)S(1)}, f32[64,640]{1,0:T(8,128)S(1)}, u32[]{:S(2)}, u32[]{:S(2)}) %collective-permute-start.31) | collective-permute-done | bytes 163872 | tf_op jit(solution)/shard_map/ppermute | solution.py:12
  160.5 6.2 %collective-permute-start.33 = (f32[64,640]{1,0:T(8,128)S(1)}, f32[64,640]{1,0:T(8,128)S(1)}, u32[]{:S(2)}, u32[]{:S(2)}) collective-permute-start(f32[64,640]{1,0:T(8,128)S(1)} %get-tuple-element.31), channel_id=1, source_target_pairs={{0,2},{2,4},{4,6},{6,8},{8,10},{10,12},{12,14},{14,16},{16,18},{18... | collective-permute-start | bytes 491528 | tf_op jit(solution)/shard_map/ppermute | solution.py:18
  166.7 3.5 %collective-permute-start.32 = (f32[64,640]{1,0:T(8,128)S(1)}, f32[64,640]{1,0:T(8,128)S(1)}, u32[]{:S(2)}, u32[]{:S(2)}) collective-permute-start(f32[64,640]{1,0:T(8,128)S(1)} %collective-permute-done.31), channel_id=1, source_target_pairs={{0,2},{2,4},{4,6},{6,8},{8,10},{10,12},{12,14},{14,16},{16,18},{18... | collective-permute-start | bytes 491528 | tf_op jit(solution)/shard_map/ppermute | solution.py:18
  170.2 5.0 %collective-permute-start.35 = (f32[64,640]{1,0:T(8,128)S(1)}, f32[64,640]{1,0:T(8,128)S(1)}, u32[]{:S(2)}, u32[]{:S(2)}) collective-permute-start(f32[64,640]{1,0:T(8,128)S(1)} %collective-permute-done.34), channel_id=1, source_target_pairs={{0,2},{2,4},{4,6},{6,8},{8,10},{10,12},{12,14},{14,16},{16,18},{18... | collective-permute-start | bytes 491528 | tf_op jit(solution)/shard_map/ppermute | solution.py:18
  179.0 11.7 %gather_fusion = f32[2048,640]{1,0:T(8,128)} fusion(f32[1024,640]{1,0:T(8,128)} %pad_maximum_fusion, s32[2048]{0:T(1024)S(1)} %get-tuple-element.39), kind=kCustom, calls=%fused_computation.2 | custom fusion | bytes 10493952 | tf_op jit(solution)/shard_map/jit(_take)/gather | solution.py:63
  190.6 5.6 %fusion = f32[4,640,128]{1,2,0:T(8,128)S(1)} fusion(f32[4,512,640]{2,1,0:T(8,128)} %bitcast.161, pred[4,512]{1,0:T(4,128)(4,1)S(1)} %compare_and_fusion, f32[1,1,4,128,512]{4,3,2,1,0:T(8,128)S(1)} %copy-done), kind=kOutput, calls=%fused_computation.8 | convolution fusion | flops 2014576640 | bytes 7604224 | tf_op jit(solution)/shard_map/bgc,bcf->bgf/dot_general | solution.py:37
  196.3 2.6 gather_fusion.3
  201.2 3.4 %collective-permute-done.36 = f32[64,640]{1,0:T(8,128)S(1)} collective-permute-done((f32[64,640]{1,0:T(8,128)S(1)}, f32[64,640]{1,0:T(8,128)S(1)}, u32[]{:S(2)}, u32[]{:S(2)}) %collective-permute-start.36) | collective-permute-done | bytes 163872 | tf_op jit(solution)/shard_map/ppermute | solution.py:12
  206.6 1.9 collective-permute-start.38
  210.8 3.2 %collective-permute-done.37 = f32[64,640]{1,0:T(8,128)S(1)} collective-permute-done((f32[64,640]{1,0:T(8,128)S(1)}, f32[64,640]{1,0:T(8,128)S(1)}, u32[]{:S(2)}, u32[]{:S(2)}) %collective-permute-start.37) | collective-permute-done | bytes 163872 | tf_op jit(solution)/shard_map/ppermute | solution.py:18
  216.2 1.9 collective-permute-start.40
  218.1 5.4 %collective-permute-done.43 = f32[64,640]{1,0:T(8,128)S(1)} collective-permute-done((f32[64,640]{1,0:T(8,128)S(1)}, f32[64,640]{1,0:T(8,128)S(1)}, u32[]{:S(2)}, u32[]{:S(2)}) %collective-permute-start.43) | collective-permute-done | bytes 163872 | tf_op jit(solution)/shard_map/ppermute | solution.py:12
  223.6 8.7 %collective-permute-start.45 = (f32[64,640]{1,0:T(8,128)S(1)}, f32[64,640]{1,0:T(8,128)S(1)}, u32[]{:S(2)}, u32[]{:S(2)}) collective-permute-start(f32[64,640]{1,0:T(8,128)S(1)} %get-tuple-element.23), channel_id=1, source_target_pairs={{0,2},{2,4},{4,6},{6,8},{8,10},{10,12},{12,14},{14,16},{16,18},{18... | collective-permute-start | bytes 491528 | tf_op jit(solution)/shard_map/ppermute | solution.py:18
  232.3 3.0 %collective-permute-start.44 = (f32[64,640]{1,0:T(8,128)S(1)}, f32[64,640]{1,0:T(8,128)S(1)}, u32[]{:S(2)}, u32[]{:S(2)}) collective-permute-start(f32[64,640]{1,0:T(8,128)S(1)} %collective-permute-done.43), channel_id=1, source_target_pairs={{0,2},{2,4},{4,6},{6,8},{8,10},{10,12},{12,14},{14,16},{16,18},{18... | collective-permute-start | bytes 491528 | tf_op jit(solution)/shard_map/ppermute | solution.py:18
  235.3 3.9 %collective-permute-start.47 = (f32[64,640]{1,0:T(8,128)S(1)}, f32[64,640]{1,0:T(8,128)S(1)}, u32[]{:S(2)}, u32[]{:S(2)}) collective-permute-start(f32[64,640]{1,0:T(8,128)S(1)} %collective-permute-done.46), channel_id=1, source_target_pairs={{0,2},{2,4},{4,6},{6,8},{8,10},{10,12},{12,14},{14,16},{16,18},{18... | collective-permute-start | bytes 491528 | tf_op jit(solution)/shard_map/ppermute | solution.py:18
  239.4 2.1 collective-permute-done.47
  243.2 7.9 %gather_fusion.1 = f32[1536,640]{1,0:T(8,128)} fusion(f32[1024,640]{1,0:T(8,128)} %pad_maximum_fusion.1, s32[2048]{0:T(1024)S(1)} %get-tuple-element.38), kind=kCustom, calls=%fused_computation.3 | custom fusion | bytes 7870464 | tf_op jit(solution)/shard_map/jit(_take)/gather | solution.py:63
  251.1 5.5 %fusion.2 = f32[4,640,128]{1,2,0:T(8,128)S(1)} fusion(f32[4,384,640]{2,1,0:T(8,128)} %bitcast.162, pred[4,384]{1,0:T(4,128)(4,1)S(1)} %compare_and_fusion.1, f32[1,1,4,128,384]{4,3,2,1,0:T(8,128)S(1)} %copy-done.1), kind=kOutput, calls=%fused_computation.10 | convolution fusion | flops 1510932480 | bytes 6030848 | tf_op jit(solution)/shard_map/bgc,bcf->bgf/dot_general | solution.py:37
  (139 shorter events, 48.1 us)
Async XLA Ops:
  22.5 8.4 %collective-permute-start = (f32[64,640]{1,0:T(8,128)S(1)}, f32[64,640]{1,0:T(8,128)S(1)}, u32[]{:S(2)}, u32[]{:S(2)}) collective-permute-start(f32[64,640]{1,0:T(8,128)S(1)} %get-tuple-element.21), channel_id=1, source_target_pairs={{0,1},{1,0},{2,3},{3,2},{4,5},{5,4},{6,7},{7,6},{8,9},{9,8},{10,11... | collective-permute-start | bytes 491528 | tf_op jit(solution)/shard_map/ppermute | solution.py:12
  24.6 12.1 %collective-permute-start.2 = (f32[64,640]{1,0:T(8,128)S(1)}, f32[64,640]{1,0:T(8,128)}, u32[]{:S(2)}, u32[]{:S(2)}) collective-permute-start(f32[64,640]{1,0:T(8,128)S(1)} %get-tuple-element.20), channel_id=1, source_target_pairs={{0,2},{2,4},{4,6},{6,8},{8,10},{10,12},{12,14},{14,16},{16,18},{18... | collective-permute-start | bytes 491528 | tf_op jit(solution)/shard_map/ppermute | solution.py:18
  28.6 8.6 %collective-permute-start.3 = (f32[64,640]{1,0:T(8,128)S(1)}, f32[64,640]{1,0:T(8,128)}, u32[]{:S(2)}, u32[]{:S(2)}) collective-permute-start(f32[64,640]{1,0:T(8,128)S(1)} %get-tuple-element.19), channel_id=1, source_target_pairs={{0,1},{1,0},{2,3},{3,2},{4,5},{5,4},{6,7},{7,6},{8,9},{9,8},{10,11... | collective-permute-start | bytes 491528 | tf_op jit(solution)/shard_map/ppermute | solution.py:12
  28.9 23.2 %collective-permute-start.5 = (f32[64,640]{1,0:T(8,128)S(1)}, f32[64,640]{1,0:T(8,128)}, u32[]{:S(2)}, u32[]{:S(2)}) collective-permute-start(f32[64,640]{1,0:T(8,128)S(1)} %get-tuple-element.18), channel_id=1, source_target_pairs={{0,1},{1,0},{2,3},{3,2},{4,5},{5,4},{6,7},{7,6},{8,9},{9,8},{10,11... | collective-permute-start | bytes 491528 | tf_op jit(solution)/shard_map/ppermute | solution.py:12
  30.1 23.0 %collective-permute-start.6 = (f32[64,640]{1,0:T(8,128)S(1)}, f32[64,640]{1,0:T(8,128)}, u32[]{:S(2)}, u32[]{:S(2)}) collective-permute-start(f32[64,640]{1,0:T(8,128)S(1)} %get-tuple-element.17), channel_id=1, source_target_pairs={{0,1},{1,0},{2,3},{3,2},{4,5},{5,4},{6,7},{7,6},{8,9},{9,8},{10,11... | collective-permute-start | bytes 491528 | tf_op jit(solution)/shard_map/ppermute | solution.py:12
  30.9 4.7 %collective-permute-start.1 = (f32[64,640]{1,0:T(8,128)S(1)}, f32[64,640]{1,0:T(8,128)S(1)}, u32[]{:S(2)}, u32[]{:S(2)}) collective-permute-start(f32[64,640]{1,0:T(8,128)S(1)} %collective-permute-done), channel_id=1, source_target_pairs={{0,2},{2,4},{4,6},{6,8},{8,10},{10,12},{12,14},{14,16},{16,18},{18... | collective-permute-start | bytes 491528 | tf_op jit(solution)/shard_map/ppermute | solution.py:18
  35.6 9.8 %collective-permute-start.7 = (f32[64,640]{1,0:T(8,128)S(1)}, f32[64,640]{1,0:T(8,128)S(1)}, u32[]{:S(2)}, u32[]{:S(2)}) collective-permute-start(f32[64,640]{1,0:T(8,128)S(1)} %get-tuple-element.16), channel_id=1, source_target_pairs={{0,1},{1,0},{2,3},{3,2},{4,5},{5,4},{6,7},{7,6},{8,9},{9,8},{10,11... | collective-permute-start | bytes 491528 | tf_op jit(solution)/shard_map/ppermute | solution.py:12
  36.7 11.4 %collective-permute-start.10 = (f32[64,640]{1,0:T(8,128)S(1)}, f32[64,640]{1,0:T(8,128)S(1)}, u32[]{:S(2)}, u32[]{:S(2)}) collective-permute-start(f32[64,640]{1,0:T(8,128)S(1)} %get-tuple-element.14), channel_id=1, source_target_pairs={{0,1},{1,0},{2,3},{3,2},{4,5},{5,4},{6,7},{7,6},{8,9},{9,8},{10,11... | collective-permute-start | bytes 491528 | tf_op jit(solution)/shard_map/ppermute | solution.py:12
  37.2 13.0 %collective-permute-start.4 = (f32[64,640]{1,0:T(8,128)}, f32[64,640]{1,0:T(8,128)S(1)}, u32[]{:S(2)}, u32[]{:S(2)}) collective-permute-start(f32[64,640]{1,0:T(8,128)} %collective-permute-done.3), channel_id=1, source_target_pairs={{0,2},{2,4},{4,6},{6,8},{8,10},{10,12},{12,14},{14,16},{16,18},{18... | collective-permute-start | bytes 491528 | tf_op jit(solution)/shard_map/ppermute | solution.py:18
  45.4 9.4 %collective-permute-start.9 = (f32[64,640]{1,0:T(8,128)S(1)}, f32[64,640]{1,0:T(8,128)S(1)}, u32[]{:S(2)}, u32[]{:S(2)}) collective-permute-start(f32[64,640]{1,0:T(8,128)S(1)} %get-tuple-element.15), channel_id=1, source_target_pairs={{2,0},{4,2},{6,4},{8,6},{10,8},{12,10},{14,12},{16,14},{18,16},{20... | collective-permute-start | bytes 491528 | tf_op jit(solution)/shard_map/ppermute | solution.py:18
  48.1 6.6 %collective-permute-start.8 = (f32[64,640]{1,0:T(8,128)S(1)}, f32[64,640]{1,0:T(8,128)S(1)}, u32[]{:S(2)}, u32[]{:S(2)}) collective-permute-start(f32[64,640]{1,0:T(8,128)S(1)} %collective-permute-done.7), channel_id=1, source_target_pairs={{2,0},{4,2},{6,4},{8,6},{10,8},{12,10},{14,12},{16,14},{18,16},{20... | collective-permute-start | bytes 491528 | tf_op jit(solution)/shard_map/ppermute | solution.py:18
  50.2 6.6 %collective-permute-start.11 = (f32[64,640]{1,0:T(8,128)S(1)}, f32[64,640]{1,0:T(8,128)S(1)}, u32[]{:S(2)}, u32[]{:S(2)}) collective-permute-start(f32[64,640]{1,0:T(8,128)S(1)} %collective-permute-done.10), channel_id=1, source_target_pairs={{2,0},{4,2},{6,4},{8,6},{10,8},{12,10},{14,12},{16,14},{18,16},{20... | collective-permute-start | bytes 491528 | tf_op jit(solution)/shard_map/ppermute | solution.py:18
  86.8 4.2 %collective-permute-start.12 = (f32[64,640]{1,0:T(8,128)S(1)}, f32[64,640]{1,0:T(8,128)S(1)}, u32[]{:S(2)}, u32[]{:S(2)}) collective-permute-start(f32[64,640]{1,0:T(8,128)S(1)} %get-tuple-element.13), channel_id=1, source_target_pairs={{0,1},{1,0},{2,3},{3,2},{4,5},{5,4},{6,7},{7,6},{8,9},{9,8},{10,11... | collective-permute-start | bytes 491528 | tf_op jit(solution)/shard_map/ppermute | solution.py:12
  91.0 8.9 %collective-permute-start.13 = (f32[64,640]{1,0:T(8,128)S(1)}, f32[64,640]{1,0:T(8,128)S(1)}, u32[]{:S(2)}, u32[]{:S(2)}) collective-permute-start(f32[64,640]{1,0:T(8,128)S(1)} %collective-permute-done.12), channel_id=1, source_target_pairs={{0,2},{2,4},{4,6},{6,8},{8,10},{10,12},{12,14},{14,16},{16,18},{18... | collective-permute-start | bytes 491528 | tf_op jit(solution)/shard_map/ppermute | solution.py:18
  94.9 7.8 %collective-permute-start.14 = (f32[64,640]{1,0:T(8,128)S(1)}, f32[64,640]{1,0:T(8,128)S(1)}, u32[]{:S(2)}, u32[]{:S(2)}) collective-permute-start(f32[64,640]{1,0:T(8,128)S(1)} %get-tuple-element.12), channel_id=1, source_target_pairs={{0,2},{2,4},{4,6},{6,8},{8,10},{10,12},{12,14},{14,16},{16,18},{18... | collective-permute-start | bytes 491528 | tf_op jit(solution)/shard_map/ppermute | solution.py:18
  98.1 6.3 %collective-permute-start.15 = (f32[64,640]{1,0:T(8,128)S(1)}, f32[64,640]{1,0:T(8,128)S(1)}, u32[]{:S(2)}, u32[]{:S(2)}) collective-permute-start(f32[64,640]{1,0:T(8,128)S(1)} %get-tuple-element.11), channel_id=1, source_target_pairs={{0,1},{1,0},{2,3},{3,2},{4,5},{5,4},{6,7},{7,6},{8,9},{9,8},{10,11... | collective-permute-start | bytes 491528 | tf_op jit(solution)/shard_map/ppermute | solution.py:12
  98.5 23.6 %collective-permute-start.17 = (f32[64,640]{1,0:T(8,128)S(1)}, f32[64,640]{1,0:T(8,128)S(1)}, u32[]{:S(2)}, u32[]{:S(2)}) collective-permute-start(f32[64,640]{1,0:T(8,128)S(1)} %get-tuple-element.10), channel_id=1, source_target_pairs={{0,1},{1,0},{2,3},{3,2},{4,5},{5,4},{6,7},{7,6},{8,9},{9,8},{10,11... | collective-permute-start | bytes 491528 | tf_op jit(solution)/shard_map/ppermute | solution.py:12
  99.6 22.5 %collective-permute-start.18 = (f32[64,640]{1,0:T(8,128)S(1)}, f32[64,640]{1,0:T(8,128)S(1)}, u32[]{:S(2)}, u32[]{:S(2)}) collective-permute-start(f32[64,640]{1,0:T(8,128)S(1)} %get-tuple-element.9), channel_id=1, source_target_pairs={{0,1},{1,0},{2,3},{3,2},{4,5},{5,4},{6,7},{7,6},{8,9},{9,8},{10,11... | collective-permute-start | bytes 491528 | tf_op jit(solution)/shard_map/ppermute | solution.py:12
  100.6 14.3 %collective-permute-start.19 = (f32[64,640]{1,0:T(8,128)S(1)}, f32[64,640]{1,0:T(8,128)S(1)}, u32[]{:S(2)}, u32[]{:S(2)}) collective-permute-start(f32[64,640]{1,0:T(8,128)S(1)} %get-tuple-element.8), channel_id=1, source_target_pairs={{0,1},{1,0},{2,3},{3,2},{4,5},{5,4},{6,7},{7,6},{8,9},{9,8},{10,11... | collective-permute-start | bytes 491528 | tf_op jit(solution)/shard_map/ppermute | solution.py:12
  102.7 15.1 %collective-permute-start.22 = (f32[64,640]{1,0:T(8,128)S(1)}, f32[64,640]{1,0:T(8,128)S(1)}, u32[]{:S(2)}, u32[]{:S(2)}) collective-permute-start(f32[64,640]{1,0:T(8,128)S(1)} %get-tuple-element.6), channel_id=1, source_target_pairs={{0,1},{1,0},{2,3},{3,2},{4,5},{5,4},{6,7},{7,6},{8,9},{9,8},{10,11... | collective-permute-start | bytes 491528 | tf_op jit(solution)/shard_map/ppermute | solution.py:12
  104.3 15.7 %collective-permute-start.16 = (f32[64,640]{1,0:T(8,128)S(1)}, f32[64,640]{1,0:T(8,128)S(1)}, u32[]{:S(2)}, u32[]{:S(2)}) collective-permute-start(f32[64,640]{1,0:T(8,128)S(1)} %collective-permute-done.15), channel_id=1, source_target_pairs={{0,2},{2,4},{4,6},{6,8},{8,10},{10,12},{12,14},{14,16},{16,18},{18... | collective-permute-start | bytes 491528 | tf_op jit(solution)/shard_map/ppermute | solution.py:18
  114.9 10.6 %collective-permute-start.21 = (f32[64,640]{1,0:T(8,128)S(1)}, f32[64,640]{1,0:T(8,128)S(1)}, u32[]{:S(2)}, u32[]{:S(2)}) collective-permute-start(f32[64,640]{1,0:T(8,128)S(1)} %get-tuple-element.7), channel_id=1, source_target_pairs={{2,0},{4,2},{6,4},{8,6},{10,8},{12,10},{14,12},{16,14},{18,16},{20... | collective-permute-start | bytes 491528 | tf_op jit(solution)/shard_map/ppermute | solution.py:18
  117.8 7.6 %collective-permute-start.20 = (f32[64,640]{1,0:T(8,128)S(1)}, f32[64,640]{1,0:T(8,128)S(1)}, u32[]{:S(2)}, u32[]{:S(2)}) collective-permute-start(f32[64,640]{1,0:T(8,128)S(1)} %collective-permute-done.19), channel_id=1, source_target_pairs={{2,0},{4,2},{6,4},{8,6},{10,8},{12,10},{14,12},{16,14},{18,16},{20... | collective-permute-start | bytes 491528 | tf_op jit(solution)/shard_map/ppermute | solution.py:18
  120.1 7.3 %collective-permute-start.23 = (f32[64,640]{1,0:T(8,128)S(1)}, f32[64,640]{1,0:T(8,128)S(1)}, u32[]{:S(2)}, u32[]{:S(2)}) collective-permute-start(f32[64,640]{1,0:T(8,128)S(1)} %collective-permute-done.22), channel_id=1, source_target_pairs={{2,0},{4,2},{6,4},{8,6},{10,8},{12,10},{14,12},{16,14},{18,16},{20... | collective-permute-start | bytes 491528 | tf_op jit(solution)/shard_map/ppermute | solution.py:18
  137.7 4.2 %collective-permute-start.24 = (f32[64,640]{1,0:T(8,128)S(1)}, f32[64,640]{1,0:T(8,128)S(1)}, u32[]{:S(2)}, u32[]{:S(2)}) collective-permute-start(f32[64,640]{1,0:T(8,128)S(1)} %get-tuple-element.37), channel_id=1, source_target_pairs={{0,1},{1,0},{2,3},{3,2},{4,5},{5,4},{6,7},{7,6},{8,9},{9,8},{10,11... | collective-permute-start | bytes 491528 | tf_op jit(solution)/shard_map/ppermute | solution.py:12
  141.9 6.9 %collective-permute-start.25 = (f32[64,640]{1,0:T(8,128)S(1)}, f32[64,640]{1,0:T(8,128)S(1)}, u32[]{:S(2)}, u32[]{:S(2)}) collective-permute-start(f32[64,640]{1,0:T(8,128)S(1)} %collective-permute-done.24), channel_id=1, source_target_pairs={{2,0},{4,2},{6,4},{8,6},{10,8},{12,10},{14,12},{16,14},{18,16},{20... | collective-permute-start | bytes 491528 | tf_op jit(solution)/shard_map/ppermute | solution.py:18
  143.9 6.9 %collective-permute-start.26 = (f32[64,640]{1,0:T(8,128)S(1)}, f32[64,640]{1,0:T(8,128)S(1)}, u32[]{:S(2)}, u32[]{:S(2)}) collective-permute-start(f32[64,640]{1,0:T(8,128)S(1)} %get-tuple-element.36), channel_id=1, source_target_pairs={{2,0},{4,2},{6,4},{8,6},{10,8},{12,10},{14,12},{16,14},{18,16},{20... | collective-permute-start | bytes 491528 | tf_op jit(solution)/shard_map/ppermute | solution.py:18
  145.8 6.3 %collective-permute-start.27 = (f32[64,640]{1,0:T(8,128)S(1)}, f32[64,640]{1,0:T(8,128)S(1)}, u32[]{:S(2)}, u32[]{:S(2)}) collective-permute-start(f32[64,640]{1,0:T(8,128)S(1)} %get-tuple-element.35), channel_id=1, source_target_pairs={{0,1},{1,0},{2,3},{3,2},{4,5},{5,4},{6,7},{7,6},{8,9},{9,8},{10,11... | collective-permute-start | bytes 491528 | tf_op jit(solution)/shard_map/ppermute | solution.py:12
  146.6 28.6 %collective-permute-start.29 = (f32[64,640]{1,0:T(8,128)S(1)}, f32[64,640]{1,0:T(8,128)S(1)}, u32[]{:S(2)}, u32[]{:S(2)}) collective-permute-start(f32[64,640]{1,0:T(8,128)S(1)} %get-tuple-element.34), channel_id=1, source_target_pairs={{0,1},{1,0},{2,3},{3,2},{4,5},{5,4},{6,7},{7,6},{8,9},{9,8},{10,11... | collective-permute-start | bytes 491528 | tf_op jit(solution)/shard_map/ppermute | solution.py:12
  147.3 27.9 %collective-permute-start.30 = (f32[64,640]{1,0:T(8,128)S(1)}, f32[64,640]{1,0:T(8,128)S(1)}, u32[]{:S(2)}, u32[]{:S(2)}) collective-permute-start(f32[64,640]{1,0:T(8,128)S(1)} %get-tuple-element.33), channel_id=1, source_target_pairs={{0,1},{1,0},{2,3},{3,2},{4,5},{5,4},{6,7},{7,6},{8,9},{9,8},{10,11... | collective-permute-start | bytes 491528 | tf_op jit(solution)/shard_map/ppermute | solution.py:12
  148.9 11.6 %collective-permute-start.31 = (f32[64,640]{1,0:T(8,128)S(1)}, f32[64,640]{1,0:T(8,128)S(1)}, u32[]{:S(2)}, u32[]{:S(2)}) collective-permute-start(f32[64,640]{1,0:T(8,128)S(1)} %get-tuple-element.32), channel_id=1, source_target_pairs={{0,1},{1,0},{2,3},{3,2},{4,5},{5,4},{6,7},{7,6},{8,9},{9,8},{10,11... | collective-permute-start | bytes 491528 | tf_op jit(solution)/shard_map/ppermute | solution.py:12
  150.8 15.9 %collective-permute-start.34 = (f32[64,640]{1,0:T(8,128)S(1)}, f32[64,640]{1,0:T(8,128)S(1)}, u32[]{:S(2)}, u32[]{:S(2)}) collective-permute-start(f32[64,640]{1,0:T(8,128)S(1)} %get-tuple-element.30), channel_id=1, source_target_pairs={{0,1},{1,0},{2,3},{3,2},{4,5},{5,4},{6,7},{7,6},{8,9},{9,8},{10,11... | collective-permute-start | bytes 491528 | tf_op jit(solution)/shard_map/ppermute | solution.py:12
  152.1 18.1 %collective-permute-start.28 = (f32[64,640]{1,0:T(8,128)S(1)}, f32[64,640]{1,0:T(8,128)S(1)}, u32[]{:S(2)}, u32[]{:S(2)}) collective-permute-start(f32[64,640]{1,0:T(8,128)S(1)} %collective-permute-done.27), channel_id=1, source_target_pairs={{2,0},{4,2},{6,4},{8,6},{10,8},{12,10},{14,12},{16,14},{18,16},{20... | collective-permute-start | bytes 491528 | tf_op jit(solution)/shard_map/ppermute | solution.py:18
  160.5 14.9 %collective-permute-start.33 = (f32[64,640]{1,0:T(8,128)S(1)}, f32[64,640]{1,0:T(8,128)S(1)}, u32[]{:S(2)}, u32[]{:S(2)}) collective-permute-start(f32[64,640]{1,0:T(8,128)S(1)} %get-tuple-element.31), channel_id=1, source_target_pairs={{0,2},{2,4},{4,6},{6,8},{8,10},{10,12},{12,14},{14,16},{16,18},{18... | collective-permute-start | bytes 491528 | tf_op jit(solution)/shard_map/ppermute | solution.py:18
  166.7 8.6 %collective-permute-start.32 = (f32[64,640]{1,0:T(8,128)S(1)}, f32[64,640]{1,0:T(8,128)S(1)}, u32[]{:S(2)}, u32[]{:S(2)}) collective-permute-start(f32[64,640]{1,0:T(8,128)S(1)} %collective-permute-done.31), channel_id=1, source_target_pairs={{0,2},{2,4},{4,6},{6,8},{8,10},{10,12},{12,14},{14,16},{16,18},{18... | collective-permute-start | bytes 491528 | tf_op jit(solution)/shard_map/ppermute | solution.py:18
  170.2 7.0 %collective-permute-start.35 = (f32[64,640]{1,0:T(8,128)S(1)}, f32[64,640]{1,0:T(8,128)S(1)}, u32[]{:S(2)}, u32[]{:S(2)}) collective-permute-start(f32[64,640]{1,0:T(8,128)S(1)} %collective-permute-done.34), channel_id=1, source_target_pairs={{0,2},{2,4},{4,6},{6,8},{8,10},{10,12},{12,14},{14,16},{16,18},{18... | collective-permute-start | bytes 491528 | tf_op jit(solution)/shard_map/ppermute | solution.py:18
  200.4 4.2 %collective-permute-start.36 = (f32[64,640]{1,0:T(8,128)S(1)}, f32[64,640]{1,0:T(8,128)S(1)}, u32[]{:S(2)}, u32[]{:S(2)}) collective-permute-start(f32[64,640]{1,0:T(8,128)S(1)} %get-tuple-element.29), channel_id=1, source_target_pairs={{0,1},{1,0},{2,3},{3,2},{4,5},{5,4},{6,7},{7,6},{8,9},{9,8},{10,11... | collective-permute-start | bytes 491528 | tf_op jit(solution)/shard_map/ppermute | solution.py:12
  204.7 9.3 %collective-permute-start.37 = (f32[64,640]{1,0:T(8,128)S(1)}, f32[64,640]{1,0:T(8,128)S(1)}, u32[]{:S(2)}, u32[]{:S(2)}) collective-permute-start(f32[64,640]{1,0:T(8,128)S(1)} %collective-permute-done.36), channel_id=1, source_target_pairs={{2,0},{4,2},{6,4},{8,6},{10,8},{12,10},{14,12},{16,14},{18,16},{20... | collective-permute-start | bytes 491528 | tf_op jit(solution)/shard_map/ppermute | solution.py:18
  206.6 9.3 %collective-permute-start.38 = (f32[64,640]{1,0:T(8,128)S(1)}, f32[64,640]{1,0:T(8,128)S(1)}, u32[]{:S(2)}, u32[]{:S(2)}) collective-permute-start(f32[64,640]{1,0:T(8,128)S(1)} %get-tuple-element.28), channel_id=1, source_target_pairs={{2,0},{4,2},{6,4},{8,6},{10,8},{12,10},{14,12},{16,14},{18,16},{20... | collective-permute-start | bytes 491528 | tf_op jit(solution)/shard_map/ppermute | solution.py:18
  208.5 7.6 %collective-permute-start.39 = (f32[64,640]{1,0:T(8,128)S(1)}, f32[64,640]{1,0:T(8,128)S(1)}, u32[]{:S(2)}, u32[]{:S(2)}) collective-permute-start(f32[64,640]{1,0:T(8,128)S(1)} %get-tuple-element.27), channel_id=1, source_target_pairs={{0,1},{1,0},{2,3},{3,2},{4,5},{5,4},{6,7},{7,6},{8,9},{9,8},{10,11... | collective-permute-start | bytes 491528 | tf_op jit(solution)/shard_map/ppermute | solution.py:12
  209.3 29.9 %collective-permute-start.41 = (f32[64,640]{1,0:T(8,128)S(1)}, f32[64,640]{1,0:T(8,128)S(1)}, u32[]{:S(2)}, u32[]{:S(2)}) collective-permute-start(f32[64,640]{1,0:T(8,128)S(1)} %get-tuple-element.26), channel_id=1, source_target_pairs={{0,1},{1,0},{2,3},{3,2},{4,5},{5,4},{6,7},{7,6},{8,9},{9,8},{10,11... | collective-permute-start | bytes 491528 | tf_op jit(solution)/shard_map/ppermute | solution.py:12
  210.1 29.2 %collective-permute-start.42 = (f32[64,640]{1,0:T(8,128)S(1)}, f32[64,640]{1,0:T(8,128)S(1)}, u32[]{:S(2)}, u32[]{:S(2)}) collective-permute-start(f32[64,640]{1,0:T(8,128)S(1)} %get-tuple-element.25), channel_id=1, source_target_pairs={{0,1},{1,0},{2,3},{3,2},{4,5},{5,4},{6,7},{7,6},{8,9},{9,8},{10,11... | collective-permute-start | bytes 491528 | tf_op jit(solution)/shard_map/ppermute | solution.py:12
  214.0 9.6 %collective-permute-start.43 = (f32[64,640]{1,0:T(8,128)S(1)}, f32[64,640]{1,0:T(8,128)S(1)}, u32[]{:S(2)}, u32[]{:S(2)}) collective-permute-start(f32[64,640]{1,0:T(8,128)S(1)} %get-tuple-element.24), channel_id=1, source_target_pairs={{0,1},{1,0},{2,3},{3,2},{4,5},{5,4},{6,7},{7,6},{8,9},{9,8},{10,11... | collective-permute-start | bytes 491528 | tf_op jit(solution)/shard_map/ppermute | solution.py:12
  215.9 16.3 %collective-permute-start.46 = (f32[64,640]{1,0:T(8,128)S(1)}, f32[64,640]{1,0:T(8,128)S(1)}, u32[]{:S(2)}, u32[]{:S(2)}) collective-permute-start(f32[64,640]{1,0:T(8,128)S(1)} %get-tuple-element.22), channel_id=1, source_target_pairs={{0,1},{1,0},{2,3},{3,2},{4,5},{5,4},{6,7},{7,6},{8,9},{9,8},{10,11... | collective-permute-start | bytes 491528 | tf_op jit(solution)/shard_map/ppermute | solution.py:12
  216.2 19.1 %collective-permute-start.40 = (f32[64,640]{1,0:T(8,128)S(1)}, f32[64,640]{1,0:T(8,128)S(1)}, u32[]{:S(2)}, u32[]{:S(2)}) collective-permute-start(f32[64,640]{1,0:T(8,128)S(1)} %collective-permute-done.39), channel_id=1, source_target_pairs={{2,0},{4,2},{6,4},{8,6},{10,8},{12,10},{14,12},{16,14},{18,16},{20... | collective-permute-start | bytes 491528 | tf_op jit(solution)/shard_map/ppermute | solution.py:18
  223.6 15.8 %collective-permute-start.45 = (f32[64,640]{1,0:T(8,128)S(1)}, f32[64,640]{1,0:T(8,128)S(1)}, u32[]{:S(2)}, u32[]{:S(2)}) collective-permute-start(f32[64,640]{1,0:T(8,128)S(1)} %get-tuple-element.23), channel_id=1, source_target_pairs={{0,2},{2,4},{4,6},{6,8},{8,10},{10,12},{12,14},{14,16},{16,18},{18... | collective-permute-start | bytes 491528 | tf_op jit(solution)/shard_map/ppermute | solution.py:18
  232.3 7.1 %collective-permute-start.44 = (f32[64,640]{1,0:T(8,128)S(1)}, f32[64,640]{1,0:T(8,128)S(1)}, u32[]{:S(2)}, u32[]{:S(2)}) collective-permute-start(f32[64,640]{1,0:T(8,128)S(1)} %collective-permute-done.43), channel_id=1, source_target_pairs={{0,2},{2,4},{4,6},{6,8},{8,10},{10,12},{12,14},{14,16},{16,18},{18... | collective-permute-start | bytes 491528 | tf_op jit(solution)/shard_map/ppermute | solution.py:18
  235.3 6.2 %collective-permute-start.47 = (f32[64,640]{1,0:T(8,128)S(1)}, f32[64,640]{1,0:T(8,128)S(1)}, u32[]{:S(2)}, u32[]{:S(2)}) collective-permute-start(f32[64,640]{1,0:T(8,128)S(1)} %collective-permute-done.46), channel_id=1, source_target_pairs={{0,2},{2,4},{4,6},{6,8},{8,10},{10,12},{12,14},{14,16},{16,18},{18... | collective-permute-start | bytes 491528 | tf_op jit(solution)/shard_map/ppermute | solution.py:18
  (11 other events, 131.3 us)
where the time goes:
time: 260 us; the launch traced here: 258 us
  starting transfers between devices  93.2 us (36%)
  waiting for transfers between devices  55.8 us (21%)
  other arithmetic  47.4 us (18%)
  local copies, waits for them, and re-layouts  36 us (14%)
  matrix products  23.9 us (9%)
    ppermute x24, starting transfers between devices, shifted(): return lax.ppermute(block, axis, route)  76.2 us
    ppermute x24, waiting for transfers between devices, passed_along(): return lax.ppermute(value, axis, pairs)  34.7 us
    scatter-add x2, other arithmetic, adjoint_blocks(): jax.ops.segment_sum(contrib.reshape(-1, values.shape[1]), cols.reshape(-1...  28.8 us
    ppermute x24, waiting for transfers between devices, shifted(): return lax.ppermute(block, axis, route)  21 us
    gather x2, local copies, waits for them, and re-layouts, apply_forward(): gathered = jnp.take(extended, cols, axis=0)  19.6 us
    ppermute x24, starting transfers between devices, passed_along(): return lax.ppermute(value, axis, pairs)  17 us
    dot_general x2, matrix products, adjoint_blocks(): jnp.einsum('bgc,bgf->bcf', weights, blocks, precision=lax.Precision.HIGHEST)  12.8 us
    dot_general x2, matrix products, block_product(): jnp.einsum('bgc,bcf->bgf', weights, gathered, precision=lax.Precision.HIG...  11.1 us
  transfers between devices with their start and end apart: 48, of which 22 were waited for; matrix products, arithmetic and copies ran while one was open for 2% of the time, Pallas kernels for 0%

commit v1 on v0

v1 whole, which is shorter than its diff:
```python
import functools

import jax
import jax.numpy as jnp
from jax import lax
from jax.experimental import pallas as pl
from jax.experimental.pallas import tpu as pltpu
from jax.sharding import PartitionSpec as P

MESH = pl.DeviceIdType.MESH
DIRECTIONS = ((-1, -1), (-1, 0), (-1, 1), (0, -1), (0, 1), (1, -1), (1, 0), (1, 1))
ORDER = (0, 2, 5, 7, 3, 4, 1, 6)
F32, BF16 = jnp.float32, jnp.bfloat16


def halves(x):
    hi = x.astype(BF16)
    return hi, (x - hi.astype(F32)).astype(BF16)


def dot(a, b):
    return jnp.dot(a, b, preferred_element_type=F32)


def dot_nt(a, b):
    return lax.dot_general(a, b, (((1,), (1,)), ((), ())), preferred_element_type=F32)


def kernel(
    n_ty, n_tx, chunks, valid_ref, ctrl_ref, iwt_ref, icols_ref, cwt_ref, ccols_ref, halo_ref,
    out_ref, imat, imat_t, cmat, cmat_t, pick, pick_t, *rest,
):
    n_chunks = len(chunks)
    send_sem, recv_sem = rest[-2:]
    buffers = rest[:-2]
    own = buffers[:n_chunks]
    rhs = buffers[n_chunks : 2 * n_chunks]
    send = [buffers[(2 + e) * n_chunks : (3 + e) * n_chunks] for e in range(4)]
    recv = [buffers[(6 + e) * n_chunks : (7 + e) * n_chunks] for e in range(4)]
    ty, tx = lax.axis_index("ty"), lax.axis_index("tx")
    rows = out_ref.shape[0]
    n_own = own[0].shape[0]
    n_slot = recv[0][0].shape[0]
    slot = n_slot // 8
    extent = n_own + n_slot

    def there(off):
        return jnp.logical_and(ty + off >= 0, ty + off < n_ty)

    def peer(row_off, col_off):
        return ty + row_off, lax.rem(tx + col_off + n_tx, n_tx)

    barrier = pltpu.get_barrier_semaphore()
    for row_off, col_off in DIRECTIONS:
        @pl.when(there(row_off))
        def _():
            pl.semaphore_signal(
                barrier, inc=1, device_id=peer(row_off, col_off), device_id_type=MESH
            )

    def copy(e, c, d):
        sign = -1 if e < 2 else 1
        row_off, col_off = DIRECTIONS[d]
        piece = pl.ds(d * slot, slot)
        return pltpu.make_async_remote_copy(
            src_ref=send[e][c].at[piece],
            dst_ref=recv[e][c].at[piece],
            send_sem=send_sem.at[e, c, d],
            recv_sem=recv_sem.at[e, c, d],
            device_id=peer(sign * row_off, sign * col_off),
            device_id_type=MESH,
        )

    def each(e, c, sending, action):
        sign = -1 if e < 2 else 1
        for d in ORDER:
            row_off = DIRECTIONS[d][0] * (sign if sending else -sign)
            if row_off == 0:
                action(copy(e, c, d))
            else:
                pl.when(there(row_off))(functools.partial(lambda e, c, d: action(copy(e, c, d)), e, c, d))

    def start(e, c):
        each(e, c, True, lambda item: item.start())

    def arrived(e, c):
        each(e, c, False, lambda item: item.wait_recv())

    def spread(wt_ref, cols_ref, mat, mat_t):
        blocks, height, width = wt_ref.shape
        for b in range(blocks):
            index = cols_ref[b : b + 1, :]
            hot = (lax.broadcasted_iota(jnp.int32, (extent, width), 0) == index).astype(F32).astype(BF16)
            hi, lo = halves(wt_ref[b])
            span = pl.ds(b * height, height)
            if mat is not None:
                mat[0, span], mat[1, span] = halves(dot_nt(hi, hot) + dot_nt(lo, hot))
            if mat_t is not None:
                mat_t[0, :, span], mat_t[1, :, span] = halves(dot_nt(hot, hi) + dot_nt(hot, lo))

    def product(mat, row0, count, col0, depth, c, base):
        a_hi = mat[0, row0 : row0 + count, col0 : col0 + depth]
        a_lo = mat[1, row0 : row0 + count, col0 : col0 + depth]
        b_hi, b_lo = rhs[c][0, base : base + depth], rhs[c][1, base : base + depth]
        return dot(a_hi, b_hi) + (dot(a_hi, b_lo) + dot(a_lo, b_hi))

    def gathered(e, c):
        hi, lo = halves(recv[e][c][...])
        return dot(pick_t[...], hi) + dot(pick_t[...], lo)

    def place(c, base, value):
        rhs[c][0, base : base + value.shape[0]], rhs[c][1, base : base + value.shape[0]] = halves(value)

    def picked(c):
        return dot(pick[...], rhs[c][0, :n_own]) + dot(pick[...], rhs[c][1, :n_own])

    for e in range(4):
        sign = -1 if e < 2 else 1
        for d, (row_off, _) in enumerate(DIRECTIONS):
            if row_off:
                @pl.when(jnp.logical_not(there(-sign * row_off)))
                def _():
                    for c in range(n_chunks):
                        piece = recv[e][c].at[pl.ds(d * slot, slot)]
                        piece[...] = jnp.zeros(piece.shape, F32)

    spread(iwt_ref, icols_ref, None, imat_t)
    limit = valid_ref[0, 0]
    edge = jnp.int32(2)
    edge += jnp.where(there(-1), 3, 0) + jnp.where(there(1), 3, 0)
    pl.semaphore_wait(barrier, edge)

    def keep(width):
        return lax.broadcasted_iota(jnp.int32, (rows, width), 0) < limit

    for c, (lo, width) in enumerate(chunks):
        place(c, 0, jnp.where(keep(width), ctrl_ref[:, lo : lo + width], 0.0))
        send[0][c][...] = product(imat_t, n_own, n_slot, 0, rows, c, 0)
        start(0, c)
        own[c][...] = product(imat_t, 0, n_own, 0, rows, c, 0)
    hot = (lax.broadcasted_iota(jnp.int32, (n_own, n_slot), 0) == halo_ref[...]).astype(F32)
    pick_t[...] = hot.astype(BF16)
    pick[...] = hot.T.astype(BF16)
    spread(cwt_ref, ccols_ref, None, cmat_t)
    for c in range(n_chunks):
        arrived(0, c)
        place(c, 0, own[c][...] + gathered(0, c))
        send[1][c][...] = product(cmat_t, n_own, n_slot, 0, n_own, c, 0)
        start(1, c)
        own[c][...] = product(cmat_t, 0, n_own, 0, n_own, c, 0)
    spread(cwt_ref, ccols_ref, cmat, None)
    spread(iwt_ref, icols_ref, imat, None)
    for c in range(n_chunks):
        arrived(1, c)
        place(c, 0, own[c][...] + gathered(1, c))
        send[2][c][...] = picked(c)
        start(2, c)
        own[c][...] = product(cmat, 0, n_own, 0, n_own, c, 0)
    for c in range(n_chunks):
        arrived(2, c)
        place(c, n_own, recv[2][c][...])
        place(c, 0, own[c][...] + product(cmat, 0, n_own, n_own, n_slot, c, n_own))
        send[3][c][...] = picked(c)
        start(3, c)
        own[c][...] = product(imat, 0, rows, 0, n_own, c, 0)
    for c, (lo, width) in enumerate(chunks):
        arrived(3, c)
        place(c, n_own, recv[3][c][...])
        total = own[c][...] + product(imat, 0, rows, n_own, n_slot, c, n_own)
        out_ref[:, lo : lo + width] = jnp.where(keep(width), total, 0.0)
    for e in range(4):
        for c in range(n_chunks):
            each(e, c, True, lambda item: item.wait_send())


def solution(mesh):
    n_ty, n_tx = mesh.shape["ty"], mesh.shape["tx"]

    def body(ctrl, interp_wt, interp_cols, conv_wt, conv_cols, halo_index, valid):
        rows, feat = ctrl.shape[2:]
        n_own = conv_wt.shape[2] * conv_wt.shape[3]
        n_slot = halo_index.shape[2] * halo_index.shape[3]
        extent = n_own + n_slot
        tiles = feat // 128
        first = 128 * max(tiles // 2, 1)
        chunks = ((0, first), (first, feat - first)) if feat > first else ((0, feat),)
        widths = [width for _, width in chunks]
        vmem = pl.BlockSpec(memory_space=pltpu.VMEM)
        scratch = [
            pltpu.VMEM((2, rows, extent), BF16),
            pltpu.VMEM((2, extent, rows), BF16),
            pltpu.VMEM((2, n_own, extent), BF16),
            pltpu.VMEM((2, extent, n_own), BF16),
            pltpu.VMEM((n_slot, n_own), BF16),
            pltpu.VMEM((n_own, n_slot), BF16),
        ]
        scratch += [pltpu.VMEM((n_own, width), F32) for width in widths]
        scratch += [pltpu.VMEM((2, extent, width), BF16) for width in widths]
        scratch += [pltpu.VMEM((n_slot, width), F32) for _ in range(8) for width in widths]
        scratch += [pltpu.SemaphoreType.DMA((4, len(chunks), 8))] * 2
        out = pl.pallas_call(
            functools.partial(kernel, n_ty, n_tx, chunks),
            out_shape=jax.ShapeDtypeStruct((rows, feat), F32),
            in_specs=[pl.BlockSpec(memory_space=pltpu.SMEM)] + [vmem] * 6,
            out_specs=vmem,
            scratch_shapes=scratch,
            compiler_params=pltpu.CompilerParams(
                collective_id=0, has_side_effects=True, vmem_limit_bytes=60 * 1024 * 1024
            ),
        )(
            valid, ctrl[0, 0], interp_wt[0, 0], interp_cols[0, 0], conv_wt[0, 0], conv_cols[0, 0],
            halo_index.reshape(1, n_slot),
        )
        return out[None, None]

    placed = (
        P("ty", "tx", None, None),
        P("ty", "tx", None, None, None),
        P("ty", "tx", None, None),
        P("ty", "tx", None, None, None),
        P("ty", "tx", None, None),
        P("ty", "tx", None, None),
        P("ty", "tx"),
    )
    return jax.shard_map(
        body, mesh=mesh, in_specs=placed, out_specs=P("ty", "tx", None, None), check_vma=False
    )
```

time: 260 us -> 101 us (0.39)
  Pallas kernels: 0 us -> 96.8 us
  starting transfers between devices: 93.2 us -> 0 us
  waiting for transfers between devices: 55.8 us -> 0 us
  other arithmetic: 47.4 us -> 0 us
  local copies, waits for them, and re-layouts: 36 us -> 3.8 us
  matrix products: 23.9 us -> 0 us
    pallas_call x0 -> x1, Pallas kernels: none -> 96.8 us  [body(): pl.pallas_call(functools.partial(kernel, n_ty, n_tx, chunks), out_shape=j...]
    ppermute x48 -> x0, starting transfers between devices: 93.2 us -> none  [the longest x24 76.2 us: shifted(): return lax.ppermute(block, axis, route)]
    ppermute x48 -> x0, waiting for transfers between devices: 55.8 us -> none  [the longest x24 34.7 us: passed_along(): return lax.ppermute(value, axis, pairs)]
    scatter-add x4 -> x0, other arithmetic: 39.2 us -> none  [the longest x2 28.8 us: adjoint_blocks(): jax.ops.segment_sum(contrib.reshape(-1, values.shape[1]), cols.reshape(-1...]
    gather x4 -> x0, local copies, waits for them, and re-layouts: 24.7 us -> none  [the longest x2 19.6 us: apply_forward(): gathered = jnp.take(extended, cols, axis=0)]
    dot_general x4 -> x0, matrix products: 23.9 us -> none  [the longest x2 12.8 us: adjoint_blocks(): jnp.einsum('bgc,bgf->bcf', weights, blocks, precision=lax.Precision.HIGHEST)]
    unnamed x48 -> x1, local copies, waits for them, and re-layouts: 7.25 us -> 2.46 us
    concatenate x2 -> x0, other arithmetic: 3.4 us -> none  [apply_forward(): extended = jnp.concatenate([owned, slots], axis=0)]
  transfers between devices with their start and end apart: 48 -> 0, of which waited for: 22 -> 0; matrix products, arithmetic and copies ran while one was open for 2% -> 0% of each run, Pallas kernels for 0% -> 0%
where the time goes in v1:
time: 101 us
  Pallas kernels  96.8 us (96%)
  local copies, waits for them, and re-layouts  3.8 us (4%)
    pallas_call x1, Pallas kernels, body(): pl.pallas_call(functools.partial(kernel, n_ty, n_tx, chunks), out_shape=j...  96.8 us
    unnamed x1, local copies, waits for them, and re-layouts  2.46 us

profile of v1, /device:TPU:1, one launch (start us, length us, event | category | flops | bytes accessed | tf_op | source)
XLA Modules:
  0.0 101.3 jit_solution(6147308333079114861)
XLA Ops:
  0.7 1.3 %reshape.3.halo_ref = s32[1,512]{1,0:T(1,128)} reshape(s32[1,1,8,64]{3,2,1,0:T(8,128)} %param.12) | data formatting | bytes 4096 | tf_op jit(solution)/shard_map/reshape | solution.py:212
  2.0 96.8 %shard_map.73 = f32[512,640]{1,0:T(8,128)} custom-call(s32[1,1]{1,0:T(1,128)S(6)} %copy.9.valid_ref, f32[512,640]{1,0:T(8,128)} %bitcast.9, f32[4,128,384]{2,1,0:T(8,128)} %bitcast.11, s32[4,384]{1,0:T(4,128)} %bitcast.13, f32[4,128,512]{2,1,0:T(8,128)} %bitcast.10, s32[4,512]{1,0:T(4,128)} %bitcast.12, s32[1,512]{1,0:T(1,128)} %reshape.3.halo_ref), custom_call_target="tpu_custom_call" | custom-call | tf_op jit(solution)/shard_map/pallas_call | solution.py:201
  98.8 2.5 %copy.10 = f32[1,1,512,640]{3,2,1,0:T(8,128)} copy(f32[1,1,512,640]{3,2,1,0:T(8,128)} %bitcast.8) | data formatting | bytes 2621440

commit v2 on v1

--- a/solution.py
+++ b/solution.py
@@ -27,16 +27,24 @@
 
 
 def kernel(
-    n_ty, n_tx, chunks, valid_ref, ctrl_ref, iwt_ref, icols_ref, cwt_ref, ccols_ref, halo_ref,
-    out_ref, imat, imat_t, cmat, cmat_t, pick, pick_t, *rest,
+    n_ty, n_tx, chunks, valid_ref, ctrl_hbm, iwt_hbm, icols_ref, cwt_hbm, ccols_ref, halo_ref,
+    out_ref, iwt_ref, cwt_ref, imat, imat_t, cmat, cmat_t, pick, pick_t, *rest,
 ):
     n_chunks = len(chunks)
-    send_sem, recv_sem = rest[-2:]
-    buffers = rest[:-2]
+    send_sem, recv_sem, load_sem, store_sem = rest[-4:]
+    buffers = rest[:-4]
     own = buffers[:n_chunks]
     rhs = buffers[n_chunks : 2 * n_chunks]
     send = [buffers[(2 + e) * n_chunks : (3 + e) * n_chunks] for e in range(4)]
     recv = [buffers[(6 + e) * n_chunks : (7 + e) * n_chunks] for e in range(4)]
+    loads = [pltpu.make_async_copy(iwt_hbm, iwt_ref, load_sem.at[0])]
+    for c, (lo, width) in enumerate(chunks):
+        loads.append(
+            pltpu.make_async_copy(ctrl_hbm.at[:, lo : lo + width], own[c], load_sem.at[1 + c])
+        )
+    loads.append(pltpu.make_async_copy(cwt_hbm, cwt_ref, load_sem.at[1 + n_chunks]))
+    for item in loads:
+        item.start()
     ty, tx = lax.axis_index("ty"), lax.axis_index("tx")
     rows = out_ref.shape[0]
     n_own = own[0].shape[0]
@@ -86,17 +94,19 @@
     def arrived(e, c):
         each(e, c, False, lambda item: item.wait_recv())
 
-    def spread(wt_ref, cols_ref, mat, mat_t):
+    def spread(wt_ref, cols_ref, mat, mat_t, base=0, count=extent):
         blocks, height, width = wt_ref.shape
         for b in range(blocks):
             index = cols_ref[b : b + 1, :]
-            hot = (lax.broadcasted_iota(jnp.int32, (extent, width), 0) == index).astype(F32).astype(BF16)
+            place_of = lax.broadcasted_iota(jnp.int32, (count, width), 0) + base
+            hot = (place_of == index).astype(F32).astype(BF16)
             hi, lo = halves(wt_ref[b])
             span = pl.ds(b * height, height)
             if mat is not None:
                 mat[0, span], mat[1, span] = halves(dot_nt(hi, hot) + dot_nt(lo, hot))
             if mat_t is not None:
-                mat_t[0, :, span], mat_t[1, :, span] = halves(dot_nt(hot, hi) + dot_nt(hot, lo))
+                part = pl.ds(base, count)
+                mat_t[0, part, span], mat_t[1, part, span] = halves(dot_nt(hot, hi) + dot_nt(hot, lo))
 
     def product(mat, row0, count, col0, depth, c, base):
         a_hi = mat[0, row0 : row0 + count, col0 : col0 + depth]
@@ -124,7 +134,8 @@
                         piece = recv[e][c].at[pl.ds(d * slot, slot)]
                         piece[...] = jnp.zeros(piece.shape, F32)
 
-    spread(iwt_ref, icols_ref, None, imat_t)
+    loads[0].wait()
+    spread(iwt_ref, icols_ref, None, imat_t, n_own, n_slot)
     limit = valid_ref[0, 0]
     edge = jnp.int32(2)
     edge += jnp.where(there(-1), 3, 0) + jnp.where(there(1), 3, 0)
@@ -134,11 +145,16 @@
         return lax.broadcasted_iota(jnp.int32, (rows, width), 0) < limit
 
     for c, (lo, width) in enumerate(chunks):
-        place(c, 0, jnp.where(keep(width), ctrl_ref[:, lo : lo + width], 0.0))
+        loads[1 + c].wait()
+        place(c, 0, jnp.where(keep(width), own[c][...], 0.0))
         send[0][c][...] = product(imat_t, n_own, n_slot, 0, rows, c, 0)
         start(0, c)
+    spread(iwt_ref, icols_ref, None, imat_t, 0, n_own)
+    for c in range(n_chunks):
         own[c][...] = product(imat_t, 0, n_own, 0, rows, c, 0)
-    hot = (lax.broadcasted_iota(jnp.int32, (n_own, n_slot), 0) == halo_ref[...]).astype(F32)
+    halo = jnp.concatenate([halo_ref[d : d + 1, :] for d in range(8)], axis=1)
+    hot = (lax.broadcasted_iota(jnp.int32, (n_own, n_slot), 0) == halo).astype(F32)
+    loads[-1].wait()
     pick_t[...] = hot.astype(BF16)
     pick[...] = hot.T.astype(BF16)
     spread(cwt_ref, ccols_ref, None, cmat_t)
@@ -163,14 +179,21 @@
         send[3][c][...] = picked(c)
         start(3, c)
         own[c][...] = product(imat, 0, rows, 0, n_own, c, 0)
+    stores = []
     for c, (lo, width) in enumerate(chunks):
         arrived(3, c)
         place(c, n_own, recv[3][c][...])
         total = own[c][...] + product(imat, 0, rows, n_own, n_slot, c, n_own)
-        out_ref[:, lo : lo + width] = jnp.where(keep(width), total, 0.0)
+        own[c][...] = jnp.where(keep(width), total, 0.0)
+        stores.append(
+            pltpu.make_async_copy(own[c], out_ref.at[:, lo : lo + width], store_sem.at[c])
+        )
+        stores[c].start()
     for e in range(4):
         for c in range(n_chunks):
             each(e, c, True, lambda item: item.wait_send())
+    for item in stores:
+        item.wait()
 
 
 def solution(mesh):
@@ -182,11 +205,15 @@
         n_slot = halo_index.shape[2] * halo_index.shape[3]
         extent = n_own + n_slot
         tiles = feat // 128
-        first = 128 * max(tiles // 2, 1)
+        first = 128 * max(tiles - tiles // 2, 1)
         chunks = ((0, first), (first, feat - first)) if feat > first else ((0, feat),)
         widths = [width for _, width in chunks]
+        pin = functools.partial(pltpu.with_memory_space_constraint, memory_space=pltpu.HBM)
+        hbm = pl.BlockSpec(memory_space=pltpu.HBM)
         vmem = pl.BlockSpec(memory_space=pltpu.VMEM)
         scratch = [
+            pltpu.VMEM(interp_wt.shape[2:], F32),
+            pltpu.VMEM(conv_wt.shape[2:], F32),
             pltpu.VMEM((2, rows, extent), BF16),
             pltpu.VMEM((2, extent, rows), BF16),
             pltpu.VMEM((2, n_own, extent), BF16),
@@ -194,22 +221,24 @@
             pltpu.VMEM((n_slot, n_own), BF16),
             pltpu.VMEM((n_own, n_slot), BF16),
         ]
+        assert rows == n_own
         scratch += [pltpu.VMEM((n_own, width), F32) for width in widths]
         scratch += [pltpu.VMEM((2, extent, width), BF16) for width in widths]
         scratch += [pltpu.VMEM((n_slot, width), F32) for _ in range(8) for width in widths]
         scratch += [pltpu.SemaphoreType.DMA((4, len(chunks), 8))] * 2
+        scratch += [pltpu.SemaphoreType.DMA((2 + len(chunks),)), pltpu.SemaphoreType.DMA((len(chunks),))]
         out = pl.pallas_call(
             functools.partial(kernel, n_ty, n_tx, chunks),
             out_shape=jax.ShapeDtypeStruct((rows, feat), F32),
-            in_specs=[pl.BlockSpec(memory_space=pltpu.SMEM)] + [vmem] * 6,
-            out_specs=vmem,
+            in_specs=[pl.BlockSpec(memory_space=pltpu.SMEM), hbm, hbm, vmem, hbm, vmem, vmem],
+            out_specs=pl.BlockSpec(memory_space=pl.ANY),
             scratch_shapes=scratch,
             compiler_params=pltpu.CompilerParams(
-                collective_id=0, has_side_effects=True, vmem_limit_bytes=60 * 1024 * 1024
+                collective_id=0, has_side_effects=True, vmem_limit_bytes=44 * 1024 * 1024
             ),
         )(
-            valid, ctrl[0, 0], interp_wt[0, 0], interp_cols[0, 0], conv_wt[0, 0], conv_cols[0, 0],
-            halo_index.reshape(1, n_slot),
+            valid, pin(ctrl[0, 0]), pin(interp_wt[0, 0]), pin(interp_cols[0, 0]), pin(conv_wt[0, 0]),
+            pin(conv_cols[0, 0]), pin(halo_index[0, 0]),
         )
         return out[None, None]
 

time: 101 us -> 96.2 us (0.952)
  local copies, waits for them, and re-layouts: 3.8 us -> 1.06 us
  Pallas kernels: 96.8 us -> 94.2 us
    pallas_call x1, Pallas kernels: 96.8 us -> 94.2 us  [body(): pl.pallas_call(functools.partial(kernel, n_ty, n_tx, chunks), out_shape=j...]
    unnamed x1, local copies, waits for them, and re-layouts: 2.46 us -> 1.06 us
    reshape x1 -> x0, local copies, waits for them, and re-layouts: 1.34 us -> none  [body(): halo_index.reshape(1, n_slot)]
where the time goes in v2:
time: 96.2 us; the launch traced here: 96 us
  Pallas kernels  94.2 us (98%)
  local copies, waits for them, and re-layouts  1.06 us (1%)
    pallas_call x1, Pallas kernels, body(): pl.pallas_call(functools.partial(kernel, n_ty, n_tx, chunks), out_shape=j...  94.2 us

profile of v2, /device:TPU:1, one launch (start us, length us, event | category | flops | bytes accessed | tf_op | source)
XLA Modules:
  0.0 96.0 jit_solution(2358142841932632508)
XLA Ops:
  0.7 94.2 %shard_map.73 = f32[512,640]{1,0:T(8,128)S(1)} custom-call(s32[1,1]{1,0:T(1,128)S(6)} %copy.9.valid_ref, f32[512,640]{1,0:T(8,128)} %bitcast.8, f32[4,128,384]{2,1,0:T(8,128)} %bitcast.10, s32[4,384]{1,0:T(4,128)} %bitcast.12, f32[4,128,512]{2,1,0:T(8,128)} %bitcast.9, s32[4,512]{1,0:T(4,128)} %bitcast.11, s32[8,64]{1,0:T(8,128)} %bitcast.13), custom_call_target="tpu_custom_call" | custom-call | tf_op jit(solution)/shard_map/pallas_call | solution.py:230
  94.9 1.1 %copy.10 = f32[1,1,512,640]{3,2,1,0:T(8,128)} copy(f32[1,1,512,640]{3,2,1,0:T(8,128)S(1)} %bitcast.7) | data formatting | bytes 2621440
